TPU v7x, 32 devices: a whole 2x2x4 slice. The times are simulated.
32 devices in a mesh: fsdp: 4 (over y, x), seq: 8 (over z, core).
Axes of the slice: x: 2, y: 2, z: 4, core: 2. Of those that a mesh axis runs over, the one named last changes fastest.
Arguments:
- images: bfloat16 [32, 1024, 1152], P('fsdp', 'seq'), may hold values from -8 to 8
- lengths: int32 [32], P('fsdp'), may hold values from 256 to 1024
- ln1_gain: bfloat16 [1152], P('fsdp'), may hold values from 0.099609375 to 1.8984375
- ln1_bias: bfloat16 [1152], P('fsdp'), may hold values from -3 to 3
- w_qkv: bfloat16 [1152, 3456], P('fsdp'), may hold values from -1 to 1
- qv_bias: bfloat16 [2, 1152], P(None, 'fsdp'), may hold values from -3 to 3
- w_out: bfloat16 [1152, 1152], P('fsdp'), may hold values from -0.75 to 0.75
- out_bias: bfloat16 [1152], P('fsdp'), may hold values from -3 to 3
- ln2_gain: bfloat16 [1152], P('fsdp'), may hold values from 0.099609375 to 1.8984375
- ln2_bias: bfloat16 [1152], P('fsdp'), may hold values from -3 to 3
- w_up: bfloat16 [1152, 4304], P('fsdp'), may hold values from -0.1875 to 0.1875
- up_bias: bfloat16 [4304], P('fsdp'), may hold values from -3 to 3
- w_down: bfloat16 [4304, 1152], P(None, 'fsdp'), may hold values from -0.09375 to 0.09375
- down_bias: bfloat16 [1152], P('fsdp'), may hold values from -3 to 3
- cotangent: bfloat16 [32, 1024, 1152], P('fsdp', 'seq'), may hold values from -6 to 6
Outputs:
- layer_out: bfloat16 [32, 1024, 1152], P('fsdp', 'seq')
- grad_images: bfloat16 [32, 1024, 1152], P('fsdp', 'seq')
- grad_ln1_gain: float32 [1152], P('fsdp')
- grad_ln1_bias: float32 [1152], P('fsdp')
- grad_w_qkv: float32 [1152, 3456], P('fsdp')
- grad_qv_bias: float32 [2, 1152], P(None, 'fsdp')
- grad_w_out: float32 [1152, 1152], P('fsdp')
- grad_out_bias: float32 [1152], P('fsdp')
- grad_ln2_gain: float32 [1152], P('fsdp')
- grad_ln2_bias: float32 [1152], P('fsdp')
- grad_w_up: float32 [1152, 4304], P('fsdp')
- grad_up_bias: float32 [4304], P('fsdp')
- grad_w_down: float32 [4304, 1152], P(None, 'fsdp')
- grad_down_bias: float32 [1152], P('fsdp')
All inputs are finite; a program needn't handle non-finite values.
Results may differ from a plain program's by a relative error of at most 0.017.
Values may be sent and summed in bfloat16 or wider, within the bound.
A program may use at most 256 MiB of HBM per device.

v0:
```python
import jax
import jax.numpy as jnp
from jax import lax
from jax.sharding import PartitionSpec as P

H = 16
HD = 72
epsilon = 1e-06
wide_block = 1024


def for_sending(shard):

    def short(part):
        return part.astype(jnp.bfloat16) if part.dtype == jnp.float32 else part

    return jax.tree.map(short, shard)


def normalize(field, gain_vec, bias_vec):
    center_mean = jnp.mean(field, -1, keepdims=True)
    centered = field - center_mean
    variance = jnp.mean(centered * centered, -1, keepdims=True)
    return centered * lax.rsqrt(variance + epsilon) * gain_vec + bias_vec


def gelu_tanh(field):
    return jax.nn.gelu(field, approximate=True)


def attend_item(queries, keys_all, values, length_one):
    length_all = keys_all.shape[1]
    block_rows = min(wide_block, length_all)
    visible = (jnp.arange(length_all) < length_one)[None, :]
    pieces = []
    log_sums = []
    for offset in range(0, length_all, block_rows):
        scores = jnp.einsum(
            "dq,dk->qk",
            queries[:, offset : offset + block_rows],
            keys_all,
            preferred_element_type=jnp.float32,
        )
        scores = jnp.where(visible, scores, -1e30)
        row_max = jnp.max(scores, -1, keepdims=True)
        exponents = jnp.exp(scores - row_max)
        denominator = jnp.sum(exponents, -1, keepdims=True)
        softmax_low = (exponents / denominator).astype(jnp.bfloat16)
        pieces.append(
            jnp.einsum("qk,dk->dq", softmax_low, values, preferred_element_type=jnp.float32)
        )
        log_sums.append(row_max[:, 0] + jnp.log(denominator[:, 0]))
    return (jnp.concatenate(pieces, 1).astype(jnp.bfloat16), jnp.concatenate(log_sums, 0))


def attend_back(queries, keys_all, values, length_one, log_sum, grad_mixed):
    length_all = keys_all.shape[1]
    block_rows = min(wide_block, length_all)
    visible = (jnp.arange(length_all) < length_one)[None, :]
    grad_keys = jnp.zeros(keys_all.shape, jnp.float32)
    grad_values = jnp.zeros(values.shape, jnp.float32)
    grad_pieces = []
    for offset in range(0, length_all, block_rows):
        query_rows = queries[:, offset : offset + block_rows]
        grad_rows = grad_mixed[:, offset : offset + block_rows]
        scores = jnp.einsum("dq,dk->qk", query_rows, keys_all, preferred_element_type=jnp.float32)
        scores = jnp.where(visible, scores, -1e30)
        softmax_out = jnp.exp(scores - log_sum[offset : offset + block_rows, None])
        grad_soft = jnp.einsum("dq,dk->qk", grad_rows, values, preferred_element_type=jnp.float32)
        row_dot = jnp.sum(softmax_out * grad_soft, -1, keepdims=True)
        grad_scores = (softmax_out * (grad_soft - row_dot)).astype(jnp.bfloat16)
        grad_pieces.append(
            jnp.einsum("qk,dk->dq", grad_scores, keys_all, preferred_element_type=jnp.float32)
        )
        grad_keys = grad_keys + jnp.einsum(
            "qk,dq->dk", grad_scores, query_rows, preferred_element_type=jnp.float32
        )
        grad_values = grad_values + jnp.einsum(
            "qk,dq->dk",
            softmax_out.astype(jnp.bfloat16),
            grad_rows,
            preferred_element_type=jnp.float32,
        )
    return (
        jnp.concatenate(grad_pieces, 1).astype(jnp.bfloat16),
        grad_keys.astype(jnp.bfloat16),
        grad_values.astype(jnp.bfloat16),
    )


def on_device(
    images,
    lengths,
    ln1_gain,
    ln1_bias,
    w_qkv,
    qv_bias,
    w_out,
    out_bias,
    ln2_gain,
    ln2_bias,
    w_up,
    up_bias,
    w_down,
    down_bias,
    cotangent,
):
    image_count, token_count, width_all = images.shape
    head_scale = HD ** (-0.5)
    gain_first, bias_first, qkv_full, qv_full, out_full, outb_full = (
        lax.all_gather(ln1_gain, "fsdp", axis=0, tiled=True),
        lax.all_gather(ln1_bias, "fsdp", axis=0, tiled=True),
        lax.all_gather(w_qkv, "fsdp", axis=0, tiled=True),
        lax.all_gather(qv_bias, "fsdp", axis=1, tiled=True),
        lax.all_gather(w_out, "fsdp", axis=0, tiled=True),
        lax.all_gather(out_bias, "fsdp", axis=0, tiled=True),
    )
    inputs_all = images.astype(jnp.float32)
    normed_first, norm_first_back = jax.vjp(
        normalize, inputs_all, gain_first.astype(jnp.float32), bias_first.astype(jnp.float32)
    )
    normed_attn = normed_first.astype(jnp.bfloat16)
    qkv_split = qkv_full.reshape(width_all, 3, H, HD)
    projected = jnp.einsum(
        "itd,dahe->ahiet", normed_attn, qkv_split, preferred_element_type=jnp.float32
    )
    shift_pair = qv_full.astype(jnp.float32).reshape(2, H, HD)
    queries = (projected[0] + shift_pair[0][:, None, :, None]) * head_scale
    values = projected[2] + shift_pair[1][:, None, :, None]
    stacked = jnp.stack([queries, projected[1], values]).astype(jnp.bfloat16)
    head_view = lax.all_to_all(stacked, "seq", split_axis=1, concat_axis=4, tiled=True)
    local_heads = head_view.shape[1]
    item_count = local_heads * image_count
    query_items = head_view[0].reshape(item_count, HD, -1)
    key_items = head_view[1].reshape(item_count, HD, -1)
    value_items = head_view[2].reshape(item_count, HD, -1)
    item_lengths = jnp.tile(lengths, local_heads)
    mixed_items, log_sums = lax.map(
        lambda packed: attend_item(*packed), (query_items, key_items, value_items, item_lengths)
    )
    mixed_tokens = lax.all_to_all(
        for_sending(mixed_items.reshape(local_heads, image_count, HD, -1)),
        "seq",
        split_axis=3,
        concat_axis=0,
        tiled=True,
    )
    out_split = out_full.reshape(H, HD, width_all)
    residual = (
        inputs_all
        + jnp.einsum("hiet,hed->itd", mixed_tokens, out_split, preferred_element_type=jnp.float32)
        + outb_full.astype(jnp.float32)
    )
    gain_second, bias_second, up_full, upb_full, down_full, downb_full = (
        lax.all_gather(ln2_gain, "fsdp", axis=0, tiled=True),
        lax.all_gather(ln2_bias, "fsdp", axis=0, tiled=True),
        lax.all_gather(w_up, "fsdp", axis=0, tiled=True),
        lax.all_gather(up_bias, "fsdp", axis=0, tiled=True),
        lax.all_gather(w_down, "fsdp", axis=1, tiled=True),
        lax.all_gather(down_bias, "fsdp", axis=0, tiled=True),
    )
    normed_second, norm_second_back = jax.vjp(
        normalize, residual, gain_second.astype(jnp.float32), bias_second.astype(jnp.float32)
    )
    normed_mlp = normed_second.astype(jnp.bfloat16)
    pre_act = jnp.einsum(
        "itd,df->itf", normed_mlp, up_full, preferred_element_type=jnp.float32
    ) + upb_full.astype(jnp.float32)
    activation, gelu_back = jax.vjp(gelu_tanh, pre_act)
    activation = activation.astype(jnp.bfloat16)
    output_all = (
        residual
        + jnp.einsum("itf,fd->itd", activation, down_full, preferred_element_type=jnp.float32)
        + downb_full.astype(jnp.float32)
    )
    layer_out = output_all.astype(jnp.bfloat16)
    qkv_back, out_back = (
        lax.all_gather(w_qkv, "fsdp", axis=0, tiled=True),
        lax.all_gather(w_out, "fsdp", axis=0, tiled=True),
    )
    up_back, down_back = (
        lax.all_gather(w_up, "fsdp", axis=0, tiled=True),
        lax.all_gather(w_down, "fsdp", axis=1, tiled=True),
    )
    grad_down = jnp.einsum("itf,itd->fd", activation, cotangent, preferred_element_type=jnp.float32)
    grad_downb = jnp.sum(cotangent, axis=(0, 1), dtype=jnp.float32)
    grad_act = jnp.einsum("itd,fd->itf", cotangent, down_back, preferred_element_type=jnp.float32)
    (grad_pre,) = gelu_back(grad_act)
    grad_pre = grad_pre.astype(jnp.bfloat16)
    grad_up = jnp.einsum("itd,itf->df", normed_mlp, grad_pre, preferred_element_type=jnp.float32)
    grad_upb = jnp.sum(grad_pre, axis=(0, 1), dtype=jnp.float32)
    grad_normed_mlp = jnp.einsum(
        "itf,df->itd", grad_pre, up_back, preferred_element_type=jnp.float32
    )
    grad_resid_norm, grad_gain_second, grad_bias_second = norm_second_back(grad_normed_mlp)
    grad_residual = cotangent.astype(jnp.float32) + grad_resid_norm
    grad_branch = grad_residual.astype(jnp.bfloat16)
    grad_outw = jnp.einsum(
        "hiet,itd->hed", mixed_tokens, grad_branch, preferred_element_type=jnp.float32
    ).reshape(width_all, width_all)
    grad_outb = jnp.sum(grad_branch, axis=(0, 1), dtype=jnp.float32)
    out_back_split = out_back.reshape(H, HD, width_all)
    grad_mixed = jnp.einsum(
        "itd,hed->hiet", grad_branch, out_back_split, preferred_element_type=jnp.float32
    ).astype(jnp.bfloat16)
    grad_head_view = lax.all_to_all(grad_mixed, "seq", split_axis=0, concat_axis=3, tiled=True)
    grad_items = grad_head_view.reshape(item_count, HD, -1)
    grad_q, grad_k, grad_v = lax.map(
        lambda packed: attend_back(*packed),
        (query_items, key_items, value_items, item_lengths, log_sums, grad_items),
    )
    grad_stack = jnp.stack([grad_q, grad_k, grad_v]).reshape(3, local_heads, image_count, HD, -1)
    grad_projected = lax.all_to_all(
        for_sending(grad_stack), "seq", split_axis=4, concat_axis=1, tiled=True
    ).astype(grad_stack.dtype)
    column_scales = jnp.array([head_scale, 1.0, 1.0], jnp.float32)
    grad_qkv = (
        jnp.einsum(
            "itd,ahiet->dahe", normed_attn, grad_projected, preferred_element_type=jnp.float32
        )
        * column_scales[None, :, None, None]
    ).reshape(width_all, 3 * width_all)
    shift_sums = jnp.sum(grad_projected, axis=(2, 4), dtype=jnp.float32)
    grad_qvb = jnp.stack([shift_sums[0] * head_scale, shift_sums[2]]).reshape(2, width_all)
    qkv_back_split = qkv_back.reshape(width_all, 3, H, HD)
    grad_normed_attn = head_scale * jnp.einsum(
        "hiet,dhe->itd", grad_projected[0], qkv_back_split[:, 0], preferred_element_type=jnp.float32
    )
    grad_normed_attn = grad_normed_attn + jnp.einsum(
        "ahiet,dahe->itd",
        grad_projected[1:],
        qkv_back_split[:, 1:],
        preferred_element_type=jnp.float32,
    )
    grad_input_norm, grad_gain_first, grad_bias_first = norm_first_back(grad_normed_attn)
    grad_images = (grad_residual + grad_input_norm).astype(jnp.bfloat16)
    (
        part_gone,
        part_bone,
        part_qkv,
        part_qvb,
        part_outw,
        part_outb,
        part_gtwo,
        part_btwo,
        part_up,
        part_upb,
        part_down,
        part_downb,
    ) = (
        lax.psum_scatter(
            grad_gain_first.astype(jnp.bfloat16), "fsdp", scatter_dimension=0, tiled=True
        ).astype(jnp.float32),
        lax.psum_scatter(
            grad_bias_first.astype(jnp.bfloat16), "fsdp", scatter_dimension=0, tiled=True
        ).astype(jnp.float32),
        lax.psum_scatter(
            grad_qkv.astype(jnp.bfloat16), "fsdp", scatter_dimension=0, tiled=True
        ).astype(jnp.float32),
        lax.psum_scatter(
            grad_qvb.astype(jnp.bfloat16), "fsdp", scatter_dimension=1, tiled=True
        ).astype(jnp.float32),
        lax.psum_scatter(
            grad_outw.astype(jnp.bfloat16), "fsdp", scatter_dimension=0, tiled=True
        ).astype(jnp.float32),
        lax.psum_scatter(
            grad_outb.astype(jnp.bfloat16), "fsdp", scatter_dimension=0, tiled=True
        ).astype(jnp.float32),
        lax.psum_scatter(
            grad_gain_second.astype(jnp.bfloat16), "fsdp", scatter_dimension=0, tiled=True
        ).astype(jnp.float32),
        lax.psum_scatter(
            grad_bias_second.astype(jnp.bfloat16), "fsdp", scatter_dimension=0, tiled=True
        ).astype(jnp.float32),
        lax.psum_scatter(
            grad_up.astype(jnp.bfloat16), "fsdp", scatter_dimension=0, tiled=True
        ).astype(jnp.float32),
        lax.psum_scatter(
            grad_upb.astype(jnp.bfloat16), "fsdp", scatter_dimension=0, tiled=True
        ).astype(jnp.float32),
        lax.psum_scatter(
            grad_down.astype(jnp.bfloat16), "fsdp", scatter_dimension=1, tiled=True
        ).astype(jnp.float32),
        lax.psum_scatter(
            grad_downb.astype(jnp.bfloat16), "fsdp", scatter_dimension=0, tiled=True
        ).astype(jnp.float32),
    )
    (
        final_gone,
        final_bone,
        final_qkv,
        final_qvb,
        final_outw,
        final_outb,
        final_gtwo,
        final_btwo,
        final_up,
        final_upb,
        final_down,
        final_downb,
    ) = (
        lax.psum(part_gone.astype(jnp.bfloat16), "seq").astype(jnp.float32),
        lax.psum(part_bone.astype(jnp.bfloat16), "seq").astype(jnp.float32),
        lax.psum(part_qkv.astype(jnp.bfloat16), "seq").astype(jnp.float32),
        lax.psum(part_qvb.astype(jnp.bfloat16), "seq").astype(jnp.float32),
        lax.psum(part_outw.astype(jnp.bfloat16), "seq").astype(jnp.float32),
        lax.psum(part_outb.astype(jnp.bfloat16), "seq").astype(jnp.float32),
        lax.psum(part_gtwo.astype(jnp.bfloat16), "seq").astype(jnp.float32),
        lax.psum(part_btwo.astype(jnp.bfloat16), "seq").astype(jnp.float32),
        lax.psum(part_up.astype(jnp.bfloat16), "seq").astype(jnp.float32),
        lax.psum(part_upb.astype(jnp.bfloat16), "seq").astype(jnp.float32),
        lax.psum(part_down.astype(jnp.bfloat16), "seq").astype(jnp.float32),
        lax.psum(part_downb.astype(jnp.bfloat16), "seq").astype(jnp.float32),
    )
    return (
        layer_out,
        grad_images,
        final_gone,
        final_bone,
        final_qkv,
        final_qvb,
        final_outw,
        final_outb,
        final_gtwo,
        final_btwo,
        final_up,
        final_upb,
        final_down,
        final_downb,
    )


def solution(mesh):
    placed = (
        P("fsdp", "seq", None),
        P("fsdp"),
        P("fsdp"),
        P("fsdp"),
        P("fsdp", None),
        P(None, "fsdp"),
        P("fsdp", None),
        P("fsdp"),
        P("fsdp"),
        P("fsdp"),
        P("fsdp", None),
        P("fsdp"),
        P(None, "fsdp"),
        P("fsdp"),
        P("fsdp", "seq", None),
    )
    return jax.shard_map(
        on_device,
        mesh=mesh,
        in_specs=placed,
        out_specs=(
            P("fsdp", "seq", None),
            P("fsdp", "seq", None),
            P("fsdp"),
            P("fsdp"),
            P("fsdp", None),
            P(None, "fsdp"),
            P("fsdp", None),
            P("fsdp"),
            P("fsdp"),
            P("fsdp"),
            P("fsdp", None),
            P("fsdp"),
            P(None, "fsdp"),
            P("fsdp"),
        ),
        check_vma=False,
    )
```

profile of v0, /device:TPU:0, one launch (start us, length us, event | category | flops | bytes accessed | tf_op | source)
XLA Modules:
  0.0 1667.9 jit_solution(1936642603031009704)
XLA Ops:
  13.0 18.5 %all-reduce.17 = (bf16[1152]{0:T(1024)(128)(2,1)S(1)}, bf16[1152]{0:T(1024)(128)(2,1)S(1)}, bf16[1152]{0:T(1024)(128)(2,1)S(1)}, bf16[1152]{0:T(1024)(128)(2,1)S...) all-reduce(bf16[1152]{0:T(1024)(128)(2,1)S(1)} %dynamic-update-slic, ...), channel_id=1, replica_groups=mesh['fsdp'=4,'seq'=8] {'fsdp'}, use_global_device_ids=true, to_apply=%add.1 | all-reduce | flops 10064 | bytes 40256
  33.3 7.5 all-gather
  41.1 55.8 %all-gather.6.cloned.1.call-done = bf16[1152,3456]{1,0:T(8,128)(2,1)} async-done(((bf16[288,3456]{1,0:T(8,128)(2,1)}), bf16[1152,3456]{1,0:T(8,128)(2,1)}) %all-gather.6.cloned.1.call-update) | async-done | bytes 7962640 | tf_op jit(solution)/shard_map/all_gather | solution.py:113
  96.9 11.5 copy.97
  108.5 12.5 convolution_bitcast_fusion.3
  123.5 4.8 copy.99
  128.3 5.0 all-to-all-start
  133.9 155.1 %all-to-all-done = bf16[3,16,8,72,128]{4,3,0,2,1:T(8,128)(2,1)} async-done(((bf16[3,16,8,72,128]{4,3,0,2,1:T(8,128)(2,1)}), bf16[3,16,8,72,128]{4,3,0,2,1:T(8,128)(2,1)}, u32[]{:S(2)}, u32[]{:S(2)}) %all-to-all-start) | async-done | bytes 7077920 | tf_op jit(solution)/shard_map/all_to_all | solution.py:131
  289.0 7.7 fusion.114
  299.6 5.0 reshape_squeeze.10
  304.6 4.6 copy.102
  309.2 4.9 reshape_squeeze.11
  314.1 4.6 copy.100
  318.7 4.9 reshape_squeeze.9
  325.3 180.0 %while.26 = (s32[]{:T(128)}, bf16[16,72,1024]{2,1,0:T(8,128)(2,1)}, f32[16,1024]{1,0:T(8,128)}, bf16[16,72,1024]{2,1,0:T(8,128)(2,1)}, s32[16]{0:T(128)S(1)}, /*...) while((s32[]{:T(128)}, bf16[16,72,1024]{2,1,0:T(8,128)(2,1)}, ...), condition=%wide.region_5.6_spmd, body=%wide.region_2.5_spmd.sunk | while | flops 311500800 | bytes 29997196 | solution.py:138
  505.4 6.3 copy.103
  511.7 4.5 all-to-all-start.1
  516.7 93.5 %all-to-all-done.1 = bf16[2,8,72,1024]{2,1,0,3:T(8,128)(2,1)} async-done(((bf16[2,8,72,1024]{2,1,0,3:T(8,128)(2,1)}), bf16[2,8,72,1024]{2,1,0,3:T(8,128)(2,1)}, u32[]{:S(2)}, u32[]{:S(2)}) %all-to-all-start.1) | async-done | bytes 2359328 | tf_op jit(solution)/shard_map/all_to_all | solution.py:141
  610.2 6.3 copy.105
  616.5 6.5 fusion.116
  625.9 24.8 %multiply_convert_fusion.1 = (bf16[8,128,4304]{1,2,0:T(8,128)(2,1)}, f32[8,128,4304]{1,2,0:T(8,128)}) fusion(f32[4304]{0:T(1024)S(1)} %convert_element_type.186, bf16[1152,4304]{1,0:T(8,128)(2,1)} %all-gather.10.cloned.1.call-done, f32[8,128,1152]{2,1,0:T(8,128)} %copy-done.5, f32[1152]{0:T(1024)S(1)} %convert_element_type.184, ...), kind=kOutput, calls=%fused_computation.72 | convolution fusion | flops 10204381184 | bytes 41113408 | tf_op jit(solution)/shard_map/itd,df->itf/dot_general | solution.py:166
  650.7 32.5 %fusion.117 = (bf16[4304]{0:T(1024)(128)(2,1)}, bf16[8,128,4304]{1,2,0:T(8,128)(2,1)}) fusion(f32[8,128,4304]{1,2,0:T(8,128)} %get-tuple-element.199, f32[4304]{0:T(1024)S(1)} %convert_element_type.186, bf16[8,128,1152]{2,1,0:T(8,128)(2,1)} %param.34, bf16[4304,1152]{0,1:T(8,128)(2,1)} %all-gather.12.cloned.1.call-done), kind=kOutput, calls=%fused_computation.155 | convolution fusion | flops 10251366400 | bytes 38745312 | tf_op jit(solution)/shard_map/itd,fd->itf/dot_general | solution.py:187
  683.2 20.6 %multiply_reduce_fusion.1 = (bf16[1152]{0:T(1024)(128)(2,1)}, f32[8,128]{1,0:T(8,128)S(1)}, bf16[1152]{0:T(1024)(128)(2,1)}, f32[8,128,1152]{2,1,0:T(8,128)}) fusion(f32[8,128,1152]{2,1,0:T(8,128)S(1)} %bitcast.254, f32[8,128]{1,0:T(8,128)S(1)} %fusion.109, f32[8,128]{1,0:T(8,128)S(1)} %broadcast_multiply_fusion, f32[1152]{0:T(1024)S(1)} %convert_element_type.183, ...), kind=kOutput, calls=%fused_computation.117 | convolution fusion | flops 10163844096 | bytes 28189696 | tf_op jit(solution)/shard_map/itf,df->itd/dot_general | solution.py:192
  710.9 4.4 fusion.71
  715.4 19.1 %fusion.54 = bf16[1152,4304]{1,0:T(8,128)(2,1)} fusion(bf16[8,128,4304]{1,2,0:T(8,128)(2,1)} %get-tuple-element.203, f32[8,128,1152]{2,1,0:T(8,128)} %copy-done.5, f32[1152]{0:T(1024)S(1)} %convert_element_type.184, f32[1152]{0:T(1024)S(1)} %convert_element_type.183, f32[8,128]{1,0:T(8,128)S(1)} %fusion.109, f32[8,128]{1,0:T(8,128)S(1)} %broadcast_multiply_fusion), kind=kOutput, calls=%fused_computation.63 | convolution fusion | flops 10165266432 | bytes 23467008 | tf_op jit(solution)/shard_map/itd,itf->df/dot_general | solution.py:190
  736.3 4.8 convert_bitcast_fusion
  747.3 16.5 fusion.55
  764.1 37.8 %all-to-all-done.2 = bf16[16,8,72,128]{3,2,1,0:T(8,128)(2,1)} async-done(((bf16[16,8,72,128]{3,2,1,0:T(8,128)(2,1)}), bf16[16,8,72,128]{3,2,1,0:T(8,128)(2,1)}, u32[]{:S(2)}, u32[]{:S(2)}) %all-to-all-start.2) | async-done | bytes 2359328 | tf_op jit(solution)/shard_map/all_to_all | solution.py:206
  811.2 220.9 %while.27 = (s32[]{:T(128)}, bf16[16,72,1024]{2,1,0:T(8,128)(2,1)S(1)}, bf16[16,72,1024]{2,1,0:T(8,128)(2,1)}, bf16[16,72,1024]{2,1,0:T(8,128)(2,1)}, bf16[16,72...) while((s32[]{:T(128)}, ...), condition=%wide.region_12.13_spmd, body=%wide.region_10.12_spmd.sunk | while | flops 767778816 | bytes 32969856 | solution.py:208
  1032.1 4.9 copy.108
  1037.0 6.4 copy.109
  1043.4 6.3 copy.110
  1049.7 6.9 pad_maximum_fusion
  1056.7 277.4 %all_to_all.66 = bf16[3,2,8,72,1024]{3,2,1,0,4:T(8,128)(2,1)} all-to-all(bf16[3,2,8,72,1024]{3,2,1,0,4:T(8,128)(2,1)S(1)} %pad_maximum_fusion), channel_id=1, replica_groups=mesh['fsdp'=4,'seq'=8] {'seq'}, dimensions={4} | all-to-all | bytes 14155776 | tf_op jit(solution)/shard_map/all_to_all | solution.py:213
  1334.1 15.4 copy.114
  1349.5 13.9 fusion.63
  1363.4 11.6 copy.115
  1376.8 13.2 copy.133
  1390.1 4.5 convert_reduce_fusion
  1405.6 5.8 fusion.98
  1411.4 8.9 fusion.110
  1424.5 17.1 %all-reduce.16 = (bf16[1152]{0:T(1024)(128)(2,1)S(1)}, bf16[1152]{0:T(1024)(128)(2,1)S(1)}, bf16[1152]{0:T(1024)(128)(2,1)S(1)}, bf16[1152]{0:T(1024)(128)(2,1)S...) all-reduce(bf16[1152]{0:T(1024)(128)(2,1)S(1)} %dynamic-update-slic, ...), channel_id=1, replica_groups=mesh['fsdp'=4,'seq'=8] {'fsdp'}, use_global_device_ids=true, to_apply=%add.6 | all-reduce | flops 12368 | bytes 49472
  1442.2 15.3 reduce-scatter.8.cloned.1.call-done
  1457.5 6.5 add_convert_fusion
  1464.1 19.0 %fusion.94 = bf16[8,128,1152]{2,1,0:T(8,128)(2,1)} fusion(f32[8,128,1152]{2,1,0:T(8,128)} %copy-done.5, bf16[8,128,4304]{1,2,0:T(8,128)(2,1)} %get-tuple-element.198, bf16[4304,1152]{0,1:T(8,128)(2,1)} %all-gather.12.cloned.1.call-done, f32[1152]{0:T(1024)S(1)} %convert_element_type.188), kind=kOutput, calls=%fused_computation.123 | convolution fusion | flops 10157948928 | bytes 25813504 | tf_op jit(solution)/shard_map/itf,fd->itd/dot_general | solution.py:173
  1486.2 29.3 %all-reduce.14 = (bf16[288]{0:T(512)(128)(2,1)S(1)}, bf16[288]{0:T(512)(128)(2,1)S(1)}, bf16[2,288]{1,0:T(2,128)(2,1)S(1)}, bf16[288]{0:T(512)(128)(2,1)S(1)}, b...) all-reduce(bf16[288]{0:T(512)(128)(2,1)S(1)} %dynamic-slice.8, ...), channel_id=1, replica_groups=mesh['fsdp'=4,'seq'=8] {'seq'}, use_global_device_ids=true, to_apply=%region_17.18 | all-reduce | flops 3380 | bytes 13520 | tf_op jit(solution)/shard_map/psum | solution.py:302
  1520.2 130.0 %all-reduce.20.cloned.1.call-done = (bf16[288,3456]{1,0:T(8,128)(2,1)}, bf16[288,1152]{1,0:T(8,128)(2,1)}, bf16[288,4304]{1,0:T(8,128)(2,1)}, bf16[4304,288]{0,1:T(8,128)(2,1)}) async-done(((bf16[288,3456]{1,0:T(8,128)(2,1)}, bf16[288,1152]{1,0:T(8,128)(2,1)}, bf16[288,4304]{1,0:T(8,128)(2,1)}, bf16[4304,288]{0,1:T(8,128)(2,1)}), (bf16[288,3456]{1,0:T(8,128)(2,1)}, bf16[288,1152]{1,0:T(8,128)(2,1)}, ...) | async-done | bytes 7612432 | tf_op jit(solution)/shard_map/psum | solution.py:304
  1650.2 4.5 convert_element_type.213
  (502 shorter events, 471.8 us)
Async XLA Ops:
  7.2 4.2 copy-start.35
  7.2 4.5 copy-start.36
  7.2 4.7 copy-start.37
  7.2 5.0 copy-start.38
  7.2 5.2 copy-start.39
  7.2 5.5 copy-start.32
  7.3 24.2 %copy-start.2 = (bf16[8,128,1152]{2,1,0:T(8,128)(2,1)S(1)}, bf16[8,128,1152]{2,1,0:T(8,128)(2,1)}, u32[]{:S(2)}) copy-start(bf16[8,128,1152]{2,1,0:T(8,128)(2,1)} %param.20) | copy-start | bytes 7077892
  7.3 26.0 %copy-start.34 = (bf16[2,288]{1,0:T(2,128)(2,1)S(1)}, bf16[2,288]{1,0:T(2,128)(2,1)}, u32[]{:S(2)}) copy-start(bf16[2,288]{1,0:T(2,128)(2,1)} %param.25) | copy-start | bytes 3460
  7.3 89.6 %all-gather.6.cloned.1.call-start = ((), (), s32[]{:S(2)}) async-start(), calls=%async_computation.9 | async-start | bytes 9953280 | tf_op jit(solution)/shard_map/all_gather | solution.py:113
  8.0 608.5 %all-gather.8.cloned.1.call-start = ((), (), s32[]{:S(2)}) async-start(), calls=%async_computation.10 | async-start | bytes 3317760 | tf_op jit(solution)/shard_map/all_gather | solution.py:115
  8.8 617.1 %all-gather.10.cloned.1.call-start = ((), (), s32[]{:S(2)}) async-start(), calls=%async_computation.11 | async-start | bytes 12533760 | tf_op jit(solution)/shard_map/all_gather | solution.py:157
  31.5 77.0 %copy-start.15 = (f32[1152]{0:T(1024)}, f32[1152]{0:T(1024)S(1)}, u32[]{:S(2)}) copy-start(f32[1152]{0:T(1024)S(1)} %convert_element_type.178) | copy-start | bytes 13828
  31.5 77.0 %copy-start.28 = (f32[1152]{0:T(1024)}, f32[1152]{0:T(1024)S(1)}, u32[]{:S(2)}) copy-start(f32[1152]{0:T(1024)S(1)} %convert_element_type.179) | copy-start | bytes 13828
  31.9 76.6 %copy-start.17 = (f32[8,128]{1,0:T(8,128)}, f32[8,128]{1,0:T(8,128)S(1)}, u32[]{:S(2)}) copy-start(f32[8,128]{1,0:T(8,128)S(1)} %broadcast_multiply_fusion.1) | copy-start | bytes 12292
  32.7 75.8 %copy-start.21 = (f32[8,128]{1,0:T(8,128)}, f32[8,128]{1,0:T(8,128)S(1)}, u32[]{:S(2)}) copy-start(f32[8,128]{1,0:T(8,128)S(1)} %fusion.108) | copy-start | bytes 12292
  128.3 5.6 copy-start.41
  128.3 160.7 %all-to-all-start = ((bf16[3,16,8,72,128]{4,3,0,2,1:T(8,128)(2,1)}), bf16[3,16,8,72,128]{4,3,0,2,1:T(8,128)(2,1)}, u32[]{:S(2)}, u32[]{:S(2)}) async-start(bf16[3,16,8,72,128]{4,3,0,2,1:T(8,128)(2,1)} %copy.99), calls=%async_computation | async-start | bytes 14155776 | tf_op jit(solution)/shard_map/all_to_all | solution.py:131
  133.2 517.4 %all-gather.12.cloned.1.call-start = ((), (), s32[]{:S(2)}) async-start(), calls=%async_computation.12 | async-start | bytes 12533760 | tf_op jit(solution)/shard_map/all_gather | solution.py:159
  505.4 6.3 copy-start.42
  511.7 98.5 %all-to-all-start.1 = ((bf16[2,8,72,1024]{2,1,0,3:T(8,128)(2,1)}), bf16[2,8,72,1024]{2,1,0,3:T(8,128)(2,1)}, u32[]{:S(2)}, u32[]{:S(2)}) async-start(bf16[2,8,72,1024]{2,1,0,3:T(8,128)(2,1)} %bitcast.255), calls=%async_computation.1 | async-start | bytes 8388608 | tf_op jit(solution)/shard_map/all_to_all | solution.py:141
  516.2 926.0 %reduce-scatter.10.cloned.1.call-start = ((), (), s32[]{:S(2)}) async-start(), calls=%async_computation.14 | async-start | bytes 3317760 | tf_op jit(solution)/shard_map/reduce_scatter | solution.py:263
  625.9 57.3 %slice-start = ((s8[4718592]{0:T(1024)(128)(4,1)}), s8[524288]{0:T(1024)(128)(4,1)S(1)}, s32[]{:S(2)}) async-start(s8[4718592]{0:T(1024)(128)(4,1)} %bitcast.253), calls=%async_computation.19 | async-start | bytes 1048576
  650.7 32.5 %slice-start.1 = ((s8[4718592]{0:T(1024)(128)(4,1)}), s8[4194304]{0:T(1024)(128)(4,1)S(1)}, s32[]{:S(2)}) async-start(s8[4718592]{0:T(1024)(128)(4,1)} %bitcast.253), calls=%async_computation.20 | async-start | bytes 8388608
  707.1 3.8 copy-start.9
  715.4 726.9 %reduce-scatter.12.cloned.1.call-start = ((), (), s32[]{:S(2)}) async-start(), calls=%async_computation.15 | async-start | bytes 12533760 | tf_op jit(solution)/shard_map/reduce_scatter | solution.py:275
  741.1 6.2 copy-start.8
  742.9 59.0 %all-to-all-start.2 = ((bf16[16,8,72,128]{3,2,1,0:T(8,128)(2,1)}), bf16[16,8,72,128]{3,2,1,0:T(8,128)(2,1)}, u32[]{:S(2)}, u32[]{:S(2)}) async-start(bf16[16,8,72,128]{3,2,1,0:T(8,128)(2,1)} %copy.106), calls=%async_computation.2 | async-start | bytes 4718592 | tf_op jit(solution)/shard_map/all_to_all | solution.py:206
  747.2 695.0 %reduce-scatter.14.cloned.1.call-start = ((), (), s32[]{:S(2)}) async-start(), calls=%async_computation.16 | async-start | bytes 12533760 | tf_op jit(solution)/shard_map/reduce_scatter | solution.py:281
  763.8 693.7 %reduce-scatter.8.cloned.1.call-start = ((), (), s32[]{:S(2)}) async-start(), calls=%async_computation.13 | async-start | bytes 9953280 | tf_op jit(solution)/shard_map/reduce_scatter | solution.py:257
  1334.0 15.4 copy-start.3
  1334.0 15.4 copy-start.16
  1334.0 15.4 copy-start.18
  1334.0 15.4 copy-start.22
  1334.0 15.4 copy-start.29
  1334.1 15.4 copy-start.44
  1375.0 110.2 %reduce-scatter.16.cloned.1.call-start = ((), (), s32[]{:S(2)}) async-start(), calls=%async_computation.17 | async-start | bytes 368640
  1390.1 5.6 copy-start.1
  1404.5 6.8 slice-start.2
  1405.6 5.8 slice-start.3
  1411.4 8.9 copy-start.24
  1420.3 4.1 copy-start.25
  1420.3 4.1 copy-start.26
  1420.3 4.1 copy-start.27
  1420.3 4.2 copy-start.30
  1420.3 4.2 copy-start.31
  1420.4 229.8 %all-reduce.20.cloned.1.call-start = ((), (), s32[]{:S(2)}) async-start(), calls=%async_computation.18 | async-start | bytes 15335424 | tf_op jit(solution)/shard_map/psum | solution.py:304
  1424.4 33.1 %copy-start.20 = (f32[8,128]{1,0:T(8,128)S(1)}, f32[8,128]{1,0:T(8,128)}, u32[]{:S(2)}) copy-start(f32[8,128]{1,0:T(8,128)} %copy-done.19) | copy-start | bytes 12292
  1650.2 4.5 copy-start.11
  (29 other events, 62.1 us)
Sparse Core Ops, SparseCore 0:
  9.9 86.9 all-gather.5
  98.8 39.7 all-gather.7
  140.4 101.0 all-gather.9
  243.3 101.0 all-gather.11
  715.5 38.3 reduce-scatter.9
  756.9 99.6 reduce-scatter.11
  859.8 99.6 reduce-scatter.13
  1375.1 82.3 reduce-scatter.7
  1460.8 24.3 reduce-scatter.15
  1487.7 162.3 all-reduce.19
where the time goes:
time: 1680 us; the launch traced here: 1670 us
  waiting for transfers between devices  492 us (29%)
  matrix products  447 us (27%)
  blocking collectives  350 us (21%)
  local copies, waits for them, and re-layouts  242 us (14%)
  other arithmetic  102 us (6%)
  between operations  18 us (1%)
    all_to_all x1, blocking collectives, on_device(): lax.all_to_all(for_sending(grad_stack), 'seq', split_axis=4, concat_axis=...  277 us
    all_to_all x1, waiting for transfers between devices, on_device(): lax.all_to_all(stacked, 'seq', split_axis=1, concat_axis=4, tiled=True)  155 us
    psum x1, waiting for transfers between devices, on_device(): lax.psum(part_qkv.astype(jnp.bfloat16), 'seq').astype(jnp.float32)  130 us
    all_to_all x1, waiting for transfers between devices, on_device(): lax.all_to_all(for_sending(mixed_items.reshape(local_heads, image_count,...  93.5 us
    dot_general x16, matrix products, attend_item(): jnp.einsum('qk,dk->dq', softmax_low, values, preferred_element_type=jnp.f...  64.5 us
    all_gather x1, waiting for transfers between devices, on_device(): lax.all_gather(w_qkv, 'fsdp', axis=0, tiled=True)  55.8 us
    dot_general x16, matrix products, attend_back(): jnp.einsum('qk,dq->dk', softmax_out.astype(jnp.bfloat16), grad_rows, pref...  42.4 us
    all_to_all x1, waiting for transfers between devices, on_device(): lax.all_to_all(grad_mixed, 'seq', split_axis=0, concat_axis=3, tiled=True)  37.8 us
  transfers between devices with their start and end apart: 13, of which 7 were waited for; matrix products, arithmetic and copies ran while one was open for 41% of the time, Pallas kernels for 0%

commit v1 on v0

--- a/solution.py
+++ b/solution.py
@@ -210,8 +210,11 @@
         (query_items, key_items, value_items, item_lengths, log_sums, grad_items),
     )
     grad_stack = jnp.stack([grad_q, grad_k, grad_v]).reshape(3, local_heads, image_count, HD, -1)
-    grad_projected = lax.all_to_all(
-        for_sending(grad_stack), "seq", split_axis=4, concat_axis=1, tiled=True
+    grad_projected = jnp.concatenate(
+        lax.all_to_all(
+            jnp.stack(jnp.split(for_sending(grad_stack), lax.axis_size("seq"), axis=4)), "seq", 0, 0
+        ),
+        axis=1,
     ).astype(grad_stack.dtype)
     column_scales = jnp.array([head_scale, 1.0, 1.0], jnp.float32)
     grad_qkv = (

time: 1680 us -> 1540 us (0.917)
  blocking collectives: 350 us -> 233 us
  local copies, waits for them, and re-layouts: 242 us -> 208 us
    all_to_all x1, blocking collectives: 277 us -> 158 us  [on_device(): lax.all_to_all(jnp.stack(jnp.split(for_sending(grad_stack), lax.axis_size...]
    all_to_all x2 -> x0, local copies, waits for them, and re-layouts: 28.6 us -> none  [on_device(): lax.all_to_all(for_sending(grad_stack), 'seq', split_axis=4, concat_axis=...]
    while x35 -> x32, local copies, waits for them, and re-layouts: 49.7 us -> 32.1 us
  transfers between devices with their start and end apart: 13 -> 13, of which waited for: 7 -> 7; matrix products, arithmetic and copies ran while one was open for 41% -> 42% of each run, Pallas kernels for 0% -> 0%
where the time goes in v1:
time: 1540 us; the launch traced here: 1520 us
  waiting for transfers between devices  505 us (33%)
  matrix products  447 us (29%)
  blocking collectives  233 us (15%)
  local copies, waits for them, and re-layouts  208 us (14%)
  other arithmetic  95.1 us (6%)
  between operations  18.1 us (1%)
    all_to_all x1, blocking collectives, on_device(): lax.all_to_all(jnp.stack(jnp.split(for_sending(grad_stack), lax.axis_size...  158 us
    all_to_all x1, waiting for transfers between devices, on_device(): lax.all_to_all(stacked, 'seq', split_axis=1, concat_axis=4, tiled=True)  155 us
    psum x1, waiting for transfers between devices, on_device(): lax.psum(part_qkv.astype(jnp.bfloat16), 'seq').astype(jnp.float32)  130 us
    all_to_all x1, waiting for transfers between devices, on_device(): lax.all_to_all(for_sending(mixed_items.reshape(local_heads, image_count,...  93.5 us
    dot_general x16, matrix products, attend_item(): jnp.einsum('qk,dk->dq', softmax_low, values, preferred_element_type=jnp.f...  64.5 us
    all_gather x1, waiting for transfers between devices, on_device(): lax.all_gather(w_qkv, 'fsdp', axis=0, tiled=True)  55.8 us
    dot_general x16, matrix products, attend_back(): jnp.einsum('qk,dq->dk', softmax_out.astype(jnp.bfloat16), grad_rows, pref...  42.4 us
    all_to_all x1, waiting for transfers between devices, on_device(): lax.all_to_all(grad_mixed, 'seq', split_axis=0, concat_axis=3, tiled=True)  37.9 us
  transfers between devices with their start and end apart: 13, of which 7 were waited for; matrix products, arithmetic and copies ran while one was open for 42% of the time, Pallas kernels for 0%

profile of v1, /device:TPU:0, one launch (start us, length us, event | category | flops | bytes accessed | tf_op | source)
XLA Modules:
  0.0 1522.3 jit_solution(12287948604341992781)
XLA Ops:
  13.0 18.5 %all-reduce.17 = (bf16[1152]{0:T(1024)(128)(2,1)S(1)}, bf16[1152]{0:T(1024)(128)(2,1)S(1)}, bf16[1152]{0:T(1024)(128)(2,1)S(1)}, bf16[1152]{0:T(1024)(128)(2,1)S...) all-reduce(bf16[1152]{0:T(1024)(128)(2,1)S(1)} %dynamic-update-slic, ...), channel_id=1, replica_groups=mesh['fsdp'=4,'seq'=8] {'fsdp'}, use_global_device_ids=true, to_apply=%add.1 | all-reduce | flops 10064 | bytes 40256
  33.3 7.5 all-gather
  41.2 55.8 %all-gather.6.cloned.1.call-done = bf16[1152,3456]{1,0:T(8,128)(2,1)} async-done(((bf16[288,3456]{1,0:T(8,128)(2,1)}), bf16[1152,3456]{1,0:T(8,128)(2,1)}) %all-gather.6.cloned.1.call-update) | async-done | bytes 7962640 | tf_op jit(solution)/shard_map/all_gather | solution.py:113
  96.9 11.6 copy.125
  108.5 12.5 convolution_bitcast_fusion.3
  123.5 4.8 copy.127
  128.3 5.0 all-to-all-start
  133.9 155.1 %all-to-all-done = bf16[3,16,8,72,128]{4,3,0,2,1:T(8,128)(2,1)} async-done(((bf16[3,16,8,72,128]{4,3,0,2,1:T(8,128)(2,1)}), bf16[3,16,8,72,128]{4,3,0,2,1:T(8,128)(2,1)}, u32[]{:S(2)}, u32[]{:S(2)}) %all-to-all-start) | async-done | bytes 7077920 | tf_op jit(solution)/shard_map/all_to_all | solution.py:131
  289.0 7.7 fusion.123
  299.6 5.0 reshape_squeeze.10
  304.6 4.6 copy.130
  309.2 4.9 reshape_squeeze.11
  314.1 4.6 copy.128
  318.7 4.9 reshape_squeeze.9
  325.4 180.0 %while.26 = (s32[]{:T(128)}, bf16[16,72,1024]{2,1,0:T(8,128)(2,1)}, f32[16,1024]{1,0:T(8,128)}, bf16[16,72,1024]{2,1,0:T(8,128)(2,1)}, s32[16]{0:T(128)S(1)}, /*...) while((s32[]{:T(128)}, bf16[16,72,1024]{2,1,0:T(8,128)(2,1)}, ...), condition=%wide.region_5.6_spmd, body=%wide.region_2.5_spmd.sunk | while | flops 311500800 | bytes 29997196 | solution.py:138
  332.6 4.0 fusion.161
  343.8 4.0 fusion.161
  366.3 4.0 fusion.161
  377.6 4.0 fusion.161
  505.4 6.3 copy.131
  511.7 4.6 all-to-all-start.1
  516.8 93.5 %all-to-all-done.1 = bf16[2,8,72,1024]{2,1,0,3:T(8,128)(2,1)} async-done(((bf16[2,8,72,1024]{2,1,0,3:T(8,128)(2,1)}), bf16[2,8,72,1024]{2,1,0,3:T(8,128)(2,1)}, u32[]{:S(2)}, u32[]{:S(2)}) %all-to-all-start.1) | async-done | bytes 2359328 | tf_op jit(solution)/shard_map/all_to_all | solution.py:141
  610.2 6.3 copy.133
  616.6 6.5 fusion.125
  625.9 24.8 %multiply_convert_fusion.1 = (bf16[8,128,4304]{1,2,0:T(8,128)(2,1)}, f32[8,128,4304]{1,2,0:T(8,128)}) fusion(f32[4304]{0:T(1024)S(1)} %convert_element_type.186, bf16[1152,4304]{1,0:T(8,128)(2,1)} %all-gather.10.cloned.1.call-done, f32[8,128,1152]{2,1,0:T(8,128)} %copy-done.5, f32[1152]{0:T(1024)S(1)} %convert_element_type.184, ...), kind=kOutput, calls=%fused_computation.72 | convolution fusion | flops 10204381184 | bytes 41113408 | tf_op jit(solution)/shard_map/itd,df->itf/dot_general | solution.py:166
  650.7 32.5 %fusion.126 = (bf16[4304]{0:T(1024)(128)(2,1)}, bf16[8,128,4304]{1,2,0:T(8,128)(2,1)}) fusion(f32[8,128,4304]{1,2,0:T(8,128)} %get-tuple-element.199, f32[4304]{0:T(1024)S(1)} %convert_element_type.186, bf16[8,128,1152]{2,1,0:T(8,128)(2,1)} %param.34, bf16[4304,1152]{0,1:T(8,128)(2,1)} %all-gather.12.cloned.1.call-done), kind=kOutput, calls=%fused_computation.172 | convolution fusion | flops 10251366400 | bytes 38745312 | tf_op jit(solution)/shard_map/itd,fd->itf/dot_general | solution.py:187
  683.2 20.6 %multiply_reduce_fusion.1 = (bf16[1152]{0:T(1024)(128)(2,1)}, f32[8,128]{1,0:T(8,128)S(1)}, bf16[1152]{0:T(1024)(128)(2,1)}, f32[8,128,1152]{2,1,0:T(8,128)}) fusion(f32[8,128,1152]{2,1,0:T(8,128)S(1)} %bitcast.288, f32[8,128]{1,0:T(8,128)S(1)} %fusion.118, f32[8,128]{1,0:T(8,128)S(1)} %broadcast_multiply_fusion, f32[1152]{0:T(1024)S(1)} %convert_element_type.183, ...), kind=kOutput, calls=%fused_computation.117 | convolution fusion | flops 10163844096 | bytes 28189696 | tf_op jit(solution)/shard_map/itf,df->itd/dot_general | solution.py:192
  710.8 4.4 fusion.71
  715.4 19.2 %fusion.54 = bf16[1152,4304]{1,0:T(8,128)(2,1)} fusion(bf16[8,128,4304]{1,2,0:T(8,128)(2,1)} %get-tuple-element.203, f32[8,128,1152]{2,1,0:T(8,128)} %copy-done.5, f32[1152]{0:T(1024)S(1)} %convert_element_type.184, f32[1152]{0:T(1024)S(1)} %convert_element_type.183, f32[8,128]{1,0:T(8,128)S(1)} %fusion.118, f32[8,128]{1,0:T(8,128)S(1)} %broadcast_multiply_fusion), kind=kOutput, calls=%fused_computation.63 | convolution fusion | flops 10165266432 | bytes 23467008 | tf_op jit(solution)/shard_map/itd,itf->df/dot_general | solution.py:190
  736.3 4.8 convert_bitcast_fusion
  742.9 4.4 all-to-all-start.2
  747.3 16.5 %fusion.55 = bf16[4304,1152]{0,1:T(8,128)(2,1)} fusion(bf16[8,128,4304]{1,2,0:T(8,128)(2,1)} %get-tuple-element.198, bf16[8,128,1152]{2,1,0:T(8,128)(2,1)S(1)} %copy-done.8), kind=kOutput, calls=%fused_computation.64 | convolution fusion | flops 10159368192 | bytes 21090304 | tf_op jit(solution)/shard_map/itf,itd->fd/dot_general | solution.py:185
  764.0 37.9 %all-to-all-done.2 = bf16[16,8,72,128]{3,2,1,0:T(8,128)(2,1)} async-done(((bf16[16,8,72,128]{3,2,1,0:T(8,128)(2,1)}), bf16[16,8,72,128]{3,2,1,0:T(8,128)(2,1)}, u32[]{:S(2)}, u32[]{:S(2)}) %all-to-all-start.2) | async-done | bytes 2359328 | tf_op jit(solution)/shard_map/all_to_all | solution.py:206
  811.3 220.8 %while.27 = (s32[]{:T(128)}, bf16[16,72,1024]{2,1,0:T(8,128)(2,1)S(1)}, bf16[16,72,1024]{2,1,0:T(8,128)(2,1)}, bf16[16,72,1024]{2,1,0:T(8,128)(2,1)}, bf16[16,72...) while((s32[]{:T(128)}, ...), condition=%wide.region_12.13_spmd, body=%wide.region_10.12_spmd.sunk | while | flops 767778816 | bytes 32969856 | solution.py:208
  1039.1 158.3 %all_to_all.53 = bf16[8,3,2,8,72,128]{5,4,2,3,1,0:T(8,128)(2,1)S(1)} all-to-all(bf16[8,3,2,8,72,128]{5,4,2,3,1,0:T(8,128)(2,1)S(1)} %copy.136), channel_id=1, replica_groups=mesh['fsdp'=4,'seq'=8] {'seq'}, dimensions={0} | all-to-all | bytes 14155776 | tf_op jit(solution)/shard_map/all_to_all | solution.py:214
  1197.4 4.6 copy.139
  1202.8 13.9 fusion.63
  1216.7 11.6 copy.140
  1233.6 5.7 slice.80
  1245.8 5.5 fusion.98
  1251.4 8.9 fusion.119
  1264.1 19.0 %all-reduce.16 = (bf16[1152]{0:T(1024)(128)(2,1)S(1)}, bf16[1152]{0:T(1024)(128)(2,1)S(1)}, bf16[1152]{0:T(1024)(128)(2,1)S(1)}, bf16[1152]{0:T(1024)(128)(2,1)S...) all-reduce(bf16[1152]{0:T(1024)(128)(2,1)S(1)} %dynamic-update-slic, ...), channel_id=1, replica_groups=mesh['fsdp'=4,'seq'=8] {'fsdp'}, use_global_device_ids=true, to_apply=%add.6 | all-reduce | flops 12368 | bytes 49472
  1283.7 28.1 %reduce-scatter.8.cloned.1.call-done = bf16[288,3456]{1,0:T(8,128)(2,1)} async-done(((bf16[1152,3456]{1,0:T(8,128)(2,1)}), bf16[288,3456]{1,0:T(8,128)(2,1)}) %reduce-scatter.8.cloned.1.call-update) | async-done | bytes 1990672 | tf_op jit(solution)/shard_map/reduce_scatter | solution.py:260
  1311.9 6.5 add_convert_fusion
  1318.4 19.0 %fusion.94 = bf16[8,128,1152]{2,1,0:T(8,128)(2,1)} fusion(f32[8,128,1152]{2,1,0:T(8,128)} %copy-done.5, bf16[8,128,4304]{1,2,0:T(8,128)(2,1)} %get-tuple-element.198, bf16[4304,1152]{0,1:T(8,128)(2,1)} %all-gather.12.cloned.1.call-done, f32[1152]{0:T(1024)S(1)} %convert_element_type.188), kind=kOutput, calls=%fused_computation.123 | convolution fusion | flops 10157948928 | bytes 25813504 | tf_op jit(solution)/shard_map/itf,fd->itd/dot_general | solution.py:173
  1340.6 29.3 %all-reduce.14 = (bf16[288]{0:T(512)(128)(2,1)S(1)}, bf16[288]{0:T(512)(128)(2,1)S(1)}, bf16[2,288]{1,0:T(2,128)(2,1)S(1)}, bf16[288]{0:T(512)(128)(2,1)S(1)}, b...) all-reduce(bf16[288]{0:T(512)(128)(2,1)S(1)} %dynamic-slice.8, ...), channel_id=1, replica_groups=mesh['fsdp'=4,'seq'=8] {'seq'}, use_global_device_ids=true, to_apply=%region_17.18 | all-reduce | flops 3380 | bytes 13520 | tf_op jit(solution)/shard_map/psum | solution.py:305
  1374.6 130.0 %all-reduce.20.cloned.1.call-done = (bf16[288,3456]{1,0:T(8,128)(2,1)}, bf16[288,1152]{1,0:T(8,128)(2,1)}, bf16[288,4304]{1,0:T(8,128)(2,1)}, bf16[4304,288]{0,1:T(8,128)(2,1)}) async-done(((bf16[288,3456]{1,0:T(8,128)(2,1)}, bf16[288,1152]{1,0:T(8,128)(2,1)}, bf16[288,4304]{1,0:T(8,128)(2,1)}, bf16[4304,288]{0,1:T(8,128)(2,1)}), (bf16[288,3456]{1,0:T(8,128)(2,1)}, bf16[288,1152]{1,0:T(8,128)(2,1)}, ...) | async-done | bytes 7612432 | tf_op jit(solution)/shard_map/psum | solution.py:307
  1504.6 4.5 convert_element_type.213
  (508 shorter events, 457.6 us)
Async XLA Ops:
  7.2 4.2 copy-start.35
  7.2 4.5 copy-start.36
  7.2 4.7 copy-start.37
  7.2 5.0 copy-start.38
  7.2 5.2 copy-start.39
  7.2 5.5 copy-start.32
  7.3 24.2 %copy-start.2 = (bf16[8,128,1152]{2,1,0:T(8,128)(2,1)S(1)}, bf16[8,128,1152]{2,1,0:T(8,128)(2,1)}, u32[]{:S(2)}) copy-start(bf16[8,128,1152]{2,1,0:T(8,128)(2,1)} %param.20) | copy-start | bytes 7077892
  7.3 26.0 %copy-start.34 = (bf16[2,288]{1,0:T(2,128)(2,1)S(1)}, bf16[2,288]{1,0:T(2,128)(2,1)}, u32[]{:S(2)}) copy-start(bf16[2,288]{1,0:T(2,128)(2,1)} %param.25) | copy-start | bytes 3460
  7.3 89.6 %all-gather.6.cloned.1.call-start = ((), (), s32[]{:S(2)}) async-start(), calls=%async_computation.9 | async-start | bytes 9953280 | tf_op jit(solution)/shard_map/all_gather | solution.py:113
  8.0 608.5 %all-gather.8.cloned.1.call-start = ((), (), s32[]{:S(2)}) async-start(), calls=%async_computation.10 | async-start | bytes 3317760 | tf_op jit(solution)/shard_map/all_gather | solution.py:115
  8.8 617.2 %all-gather.10.cloned.1.call-start = ((), (), s32[]{:S(2)}) async-start(), calls=%async_computation.11 | async-start | bytes 12533760 | tf_op jit(solution)/shard_map/all_gather | solution.py:157
  31.5 77.0 %copy-start.15 = (f32[1152]{0:T(1024)}, f32[1152]{0:T(1024)S(1)}, u32[]{:S(2)}) copy-start(f32[1152]{0:T(1024)S(1)} %convert_element_type.178) | copy-start | bytes 13828
  31.5 77.0 %copy-start.28 = (f32[1152]{0:T(1024)}, f32[1152]{0:T(1024)S(1)}, u32[]{:S(2)}) copy-start(f32[1152]{0:T(1024)S(1)} %convert_element_type.179) | copy-start | bytes 13828
  31.9 76.6 %copy-start.17 = (f32[8,128]{1,0:T(8,128)}, f32[8,128]{1,0:T(8,128)S(1)}, u32[]{:S(2)}) copy-start(f32[8,128]{1,0:T(8,128)S(1)} %broadcast_multiply_fusion.1) | copy-start | bytes 12292
  32.7 75.8 %copy-start.21 = (f32[8,128]{1,0:T(8,128)}, f32[8,128]{1,0:T(8,128)S(1)}, u32[]{:S(2)}) copy-start(f32[8,128]{1,0:T(8,128)S(1)} %fusion.117) | copy-start | bytes 12292
  128.3 5.6 copy-start.41
  128.3 160.7 %all-to-all-start = ((bf16[3,16,8,72,128]{4,3,0,2,1:T(8,128)(2,1)}), bf16[3,16,8,72,128]{4,3,0,2,1:T(8,128)(2,1)}, u32[]{:S(2)}, u32[]{:S(2)}) async-start(bf16[3,16,8,72,128]{4,3,0,2,1:T(8,128)(2,1)} %copy.127), calls=%async_computation | async-start | bytes 14155776 | tf_op jit(solution)/shard_map/all_to_all | solution.py:131
  133.3 517.4 %all-gather.12.cloned.1.call-start = ((), (), s32[]{:S(2)}) async-start(), calls=%async_computation.12 | async-start | bytes 12533760 | tf_op jit(solution)/shard_map/all_gather | solution.py:159
  505.4 6.3 copy-start.42
  511.7 98.6 %all-to-all-start.1 = ((bf16[2,8,72,1024]{2,1,0,3:T(8,128)(2,1)}), bf16[2,8,72,1024]{2,1,0,3:T(8,128)(2,1)}, u32[]{:S(2)}, u32[]{:S(2)}) async-start(bf16[2,8,72,1024]{2,1,0,3:T(8,128)(2,1)} %bitcast.289), calls=%async_computation.1 | async-start | bytes 8388608 | tf_op jit(solution)/shard_map/all_to_all | solution.py:141
  516.3 767.5 %reduce-scatter.10.cloned.1.call-start = ((), (), s32[]{:S(2)}) async-start(), calls=%async_computation.14 | async-start | bytes 3317760 | tf_op jit(solution)/shard_map/reduce_scatter | solution.py:266
  625.9 57.2 %slice-start.2 = ((s8[4718592]{0:T(1024)(128)(4,1)}), s8[524288]{0:T(1024)(128)(4,1)S(1)}, s32[]{:S(2)}) async-start(s8[4718592]{0:T(1024)(128)(4,1)} %bitcast.287), calls=%async_computation.21 | async-start | bytes 1048576
  650.7 32.5 %slice-start.3 = ((s8[4718592]{0:T(1024)(128)(4,1)}), s8[4194304]{0:T(1024)(128)(4,1)S(1)}, s32[]{:S(2)}) async-start(s8[4718592]{0:T(1024)(128)(4,1)} %bitcast.287), calls=%async_computation.22 | async-start | bytes 8388608
  715.3 568.4 %reduce-scatter.12.cloned.1.call-start = ((), (), s32[]{:S(2)}) async-start(), calls=%async_computation.15 | async-start | bytes 12533760 | tf_op jit(solution)/shard_map/reduce_scatter | solution.py:278
  741.1 6.2 copy-start.8
  742.9 59.0 %all-to-all-start.2 = ((bf16[16,8,72,128]{3,2,1,0:T(8,128)(2,1)}), bf16[16,8,72,128]{3,2,1,0:T(8,128)(2,1)}, u32[]{:S(2)}, u32[]{:S(2)}) async-start(bf16[16,8,72,128]{3,2,1,0:T(8,128)(2,1)} %copy.134), calls=%async_computation.2 | async-start | bytes 4718592 | tf_op jit(solution)/shard_map/all_to_all | solution.py:206
  747.2 536.5 %reduce-scatter.14.cloned.1.call-start = ((), (), s32[]{:S(2)}) async-start(), calls=%async_computation.16 | async-start | bytes 12533760 | tf_op jit(solution)/shard_map/reduce_scatter | solution.py:284
  763.8 548.0 %reduce-scatter.8.cloned.1.call-start = ((), (), s32[]{:S(2)}) async-start(), calls=%async_computation.13 | async-start | bytes 9953280 | tf_op jit(solution)/shard_map/reduce_scatter | solution.py:260
  1197.4 5.4 copy-start.1
  1197.4 5.4 copy-start.3
  1197.4 5.4 copy-start.16
  1197.4 5.4 copy-start.18
  1197.4 5.4 copy-start.22
  1197.4 5.4 copy-start.29
  1197.4 5.4 copy-start.44
  1228.3 111.3 %reduce-scatter.16.cloned.1.call-start = ((), (), s32[]{:S(2)}) async-start(), calls=%async_computation.17 | async-start | bytes 368640
  1230.2 9.2 slice-start
  1233.6 5.8 slice-start.1
  1244.7 6.6 slice-start.4
  1245.8 5.5 slice-start.5
  1251.3 8.9 copy-start.24
  1260.3 3.8 copy-start.26
  1260.3 3.9 copy-start.27
  1260.3 3.9 copy-start.30
  1260.3 3.9 copy-start.31
  1260.3 244.3 %all-reduce.20.cloned.1.call-start = ((), (), s32[]{:S(2)}) async-start(), calls=%async_computation.18 | async-start | bytes 15335424 | tf_op jit(solution)/shard_map/psum | solution.py:307
  1264.1 47.8 %copy-start.20 = (f32[8,128]{1,0:T(8,128)S(1)}, f32[8,128]{1,0:T(8,128)}, u32[]{:S(2)}) copy-start(f32[8,128]{1,0:T(8,128)} %copy-done.19) | copy-start | bytes 12292
  1504.6 4.5 copy-start.11
  (31 other events, 69.5 us)
Sparse Core Ops, SparseCore 0:
  9.9 86.9 all-gather.5
  98.8 39.7 all-gather.7
  140.4 101.1 all-gather.9
  243.3 101.0 all-gather.11
  715.4 38.3 reduce-scatter.9
  756.9 99.6 reduce-scatter.11
  859.8 99.6 reduce-scatter.13
  1228.4 83.3 reduce-scatter.7
  1315.2 24.4 reduce-scatter.15
  1342.2 162.3 all-reduce.19
